TPU v7x, 32 devices: a whole 2x2x4 slice. The times are simulated.
32 devices in a mesh: sector: 4 (over y, core), member: 8 (over z, x).
Axes of the slice: x: 2, y: 2, z: 4, core: 2. Of those that a mesh axis runs over, the one named last changes fastest.
Arguments:
- state: bfloat16 [16, 1024, 256], P('member', 'sector'), may hold values from -18 to 18
- window_mask: int32 [1024, 256], P('sector'), may hold values 0 or 1
- window_index: int32 [1024], replicated, may hold values from 0 to 7, never falling along the last dimension, each value on 1 to 256 neighbouring positions
- w_space_qkv: bfloat16 [256, 768], replicated, may hold values from -0.375 to 0.375
- w_space_out: bfloat16 [256, 256], replicated, may hold values from -0.375 to 0.375
- temp_space: float32 [8], replicated, may hold values from 0.5 to 64
- w_ens_qkv: bfloat16 [256, 768], replicated, may hold values from -0.375 to 0.375
- w_ens_out: bfloat16 [256, 256], replicated, may hold values from -0.375 to 0.375
- temp_ens: float32 [8], replicated, may hold values from 0.5 to 64
- w_in: bfloat16 [256, 1024], replicated, may hold values from -0.375 to 0.375
- w_out: bfloat16 [1024, 256], replicated, may hold values from -0.1875 to 0.1875
Outputs:
- out_state: bfloat16 [16, 1024, 256], P('member', 'sector')
Inputs may be any that keep to these rules, and one draw needn't show every extreme that they name: `window_index`: window numbers never fall along the patches; a window spans 1 to 256 patches.
All inputs are finite; a program needn't handle non-finite values. No bound on the sum of `window_mask` on one device may be relied on, other than what follows from the above.
Results may differ from a plain program's by a relative error of at most 0.015.
The roundings to bfloat16 on the way count: a program that leaves them out, or rounds other values in their place, can miss the bound.
Values may be sent and summed in bfloat16 or wider, within the bound.
No kernel may reach another device: no remote copies, remote signals or barrier semaphores. Data moves between devices by JAX's collectives and lax.ppermute only.
A program may use at most 64 MiB of HBM per device.

v0:
```python
import math

import jax
import jax.numpy as jnp
from jax import lax
from jax.sharding import PartitionSpec as P


def padded_2(x, sides, width):
    for axis, dim in sides:
        size, length = (lax.axis_size(axis), x.shape[dim])
        up = [(i, (i + 1) % size) for i in range(size)]
        down = [(j, i) for i, j in up]
        last = lax.slice_in_dim(x, length - width, length, axis=dim)
        first = lax.slice_in_dim(x, 0, width, axis=dim)
        before = lax.ppermute(last, axis, up)
        after = lax.ppermute(first, axis, down)
        x = jnp.concatenate([before, x, after], axis=dim)
    return x


def rms_rows(values):
    squares = jnp.mean(values * values, axis=-1, keepdims=True)
    return values * lax.rsqrt(squares + 1e-06)


def head_norm(values, total_heads):
    shaped = values.reshape(values.shape[:-1] + (total_heads, values.shape[-1] // total_heads))
    squares = jnp.mean(shaped * shaped, axis=-1, keepdims=True)
    return (shaped * lax.rsqrt(squares + 0.1)).reshape(values.shape)


def skew_band(table, span_width):
    row_count, columns = table.shape
    padded = jnp.pad(table, ((0, 0), (0, span_width + 1 - columns)))
    return padded.reshape(-1)[: row_count * span_width].reshape(row_count, span_width)


def attend_window(queries, keys, values, query_window, key_window, mask_rows, logit_scale):
    span_width = keys.shape[1]
    banded = skew_band(mask_rows + 1, span_width)
    same_window = query_window[:, None] == key_window[None, :]
    allowed = (banded == 2) | (banded == 1) & same_window
    scores = jnp.einsum("mqhd,mkhd->mhqk", queries, keys, preferred_element_type=jnp.float32)
    scores = scores * logit_scale[None, :, None, None]
    scores = jnp.where(allowed[None, None], scores, -1e30)
    row_max = jnp.max(scores, axis=-1, keepdims=True)
    exponent = jnp.exp(scores - row_max)
    weights = (exponent / jnp.sum(exponent, axis=-1, keepdims=True)).astype(jnp.bfloat16)
    return jnp.einsum("mhqk,mkhd->mqhd", weights, values, preferred_element_type=jnp.float32)


def member_attention_step(
    row_tile_size, query_key_value_weight, output_projection_weight, sampling_heat, total_heads
):
    everyone, patch_count, features = row_tile_size.shape
    head_width = features // total_heads
    normed = rms_rows(row_tile_size.astype(jnp.float32)).astype(jnp.bfloat16)
    projected = jnp.dot(
        normed.reshape(-1, features), query_key_value_weight, preferred_element_type=jnp.float32
    )
    projected = projected.reshape(everyone, patch_count, 3 * features)
    shape_heads = (everyone, patch_count, total_heads, head_width)
    query_rows = (
        head_norm(projected[..., :features], total_heads).astype(jnp.bfloat16).reshape(shape_heads)
    )
    key_rows = (
        head_norm(projected[..., features : 2 * features], total_heads)
        .astype(jnp.bfloat16)
        .reshape(shape_heads)
    )
    value_rows = projected[..., 2 * features :].astype(jnp.bfloat16).reshape(shape_heads)
    logit_scale = sampling_heat / math.sqrt(head_width)
    scores = jnp.einsum("mphd,nphd->phmn", query_rows, key_rows, preferred_element_type=jnp.float32)
    scores = scores * logit_scale[None, :, None, None]
    row_max = jnp.max(scores, axis=-1, keepdims=True)
    exponent = jnp.exp(scores - row_max)
    weights = (exponent / jnp.sum(exponent, axis=-1, keepdims=True)).astype(jnp.bfloat16)
    mixed_heads = jnp.einsum(
        "phmn,nphd->mphd", weights, value_rows, preferred_element_type=jnp.float32
    )
    mixed_heads = mixed_heads.reshape(everyone * patch_count, features).astype(jnp.bfloat16)
    update = jnp.dot(
        mixed_heads, output_projection_weight, preferred_element_type=jnp.float32
    ).reshape(row_tile_size.shape)
    return (row_tile_size.astype(jnp.float32) + update).astype(jnp.bfloat16)


def feed_forward(row_tile_size, w_in, w_out):
    features = row_tile_size.shape[-1]
    normed = rms_rows(row_tile_size.astype(jnp.float32)).astype(jnp.bfloat16).reshape(-1, features)
    hidden = jax.nn.gelu(jnp.dot(normed, w_in, preferred_element_type=jnp.float32)).astype(
        jnp.bfloat16
    )
    update = jnp.dot(hidden, w_out, preferred_element_type=jnp.float32).reshape(row_tile_size.shape)
    return (row_tile_size.astype(jnp.float32) + update).astype(jnp.bfloat16)


def on_device(
    state,
    window_mask,
    window_index,
    w_space_qkv,
    w_space_out,
    temp_space,
    w_ens_qkv,
    w_ens_out,
    temp_ens,
    w_in,
    w_out,
):
    members, tokens, features = state.shape
    total_heads = temp_space.shape[0]
    head_width = features // total_heads
    radius = window_mask.shape[1] // 2
    block_rows = min(tokens, 256)
    cycle_length = window_index.shape[0]
    first_patch = lax.axis_index("sector") * tokens
    normed = rms_rows(state.astype(jnp.float32)).astype(jnp.bfloat16)
    projected = jnp.dot(
        normed.reshape(-1, features), w_space_qkv, preferred_element_type=jnp.float32
    )
    projected = projected.reshape(members, tokens, 3 * features)
    query_rows = head_norm(projected[..., :features], total_heads).astype(jnp.bfloat16)
    key_rows = head_norm(projected[..., features : 2 * features], total_heads).astype(jnp.bfloat16)
    value_rows = projected[..., 2 * features :].astype(jnp.bfloat16)
    rimmed = padded_2(normed, (("sector", 1),), radius)
    edges = jnp.concatenate([rimmed[:, :radius], rimmed[:, tokens + radius :]], axis=1)
    edge_proj = jnp.dot(
        edges.reshape(-1, features), w_space_qkv[:, features:], preferred_element_type=jnp.float32
    )
    edge_proj = edge_proj.reshape(members, 2 * radius, 2 * features)
    edge_keys = head_norm(edge_proj[..., :features], total_heads).astype(jnp.bfloat16)
    edge_values = edge_proj[..., features:].astype(jnp.bfloat16)
    key_cycle = jnp.concatenate([edge_keys[:, :radius], key_rows, edge_keys[:, radius:]], axis=1)
    value_cycle = jnp.concatenate(
        [edge_values[:, :radius], value_rows, edge_values[:, radius:]], axis=1
    )
    cycle_index = jnp.concatenate(
        [window_index[cycle_length - radius :], window_index, window_index[:radius]]
    )
    query_heads = query_rows.reshape(members, tokens, total_heads, head_width)
    key_heads = key_cycle.reshape(members, tokens + 2 * radius, total_heads, head_width)
    value_heads = value_cycle.reshape(members, tokens + 2 * radius, total_heads, head_width)
    logit_scale = temp_space / math.sqrt(head_width)

    def one_block(offset):
        query_window = lax.dynamic_slice_in_dim(window_index, first_patch + offset, block_rows, 0)
        key_window = lax.dynamic_slice_in_dim(
            cycle_index, first_patch + offset, block_rows + 2 * radius, 0
        )
        attended = attend_window(
            query_heads, key_heads, value_heads, query_window, key_window, window_mask, logit_scale
        )
        return attended.astype(jnp.bfloat16)

    offsets = jnp.arange(tokens // block_rows, dtype=jnp.int32) * block_rows
    outputs = lax.map(one_block, offsets)
    mixed_heads = jnp.moveaxis(outputs, 0, 1).reshape(members * tokens, features)
    update = jnp.dot(mixed_heads, w_space_out, preferred_element_type=jnp.float32).reshape(
        state.shape
    )
    state_b = (state.astype(jnp.float32) + update).astype(jnp.bfloat16)
    group_size = lax.axis_size("member")
    patch_share = tokens // group_size
    regrouped = state_b.reshape(members, group_size, patch_share, features)
    parcel = lax.all_to_all(regrouped, "member", split_axis=1, concat_axis=0, tiled=True)
    everyone = parcel.shape[0]
    patch_count = parcel.shape[2]
    row_tile_size = parcel.reshape(everyone, patch_count, features)
    result = member_attention_step(row_tile_size, w_ens_qkv, w_ens_out, temp_ens, total_heads)
    gathered = result.reshape(everyone, 1, patch_count, features)
    returned = lax.all_to_all(gathered, "member", split_axis=0, concat_axis=1, tiled=True)
    state_c = returned.reshape(members, tokens, features)
    state_c = feed_forward(state_c, w_in, w_out)
    return state_c


def solution(mesh):
    return jax.shard_map(
        on_device,
        mesh=mesh,
        in_specs=(
            P("member", "sector", None),
            P("sector", None),
            P(),
            P(),
            P(),
            P(),
            P(),
            P(),
            P(),
            P(),
            P(),
        ),
        out_specs=P("member", "sector", None),
        check_vma=False,
    )
```

profile of v0, /device:TPU:0, one launch (start us, length us, event | category | flops | bytes accessed | tf_op | source)
XLA Modules:
  0.0 97.9 jit_solution(17200650717833999112)
XLA Ops:
  0.0 1.2 %fusion.34 = f32[2,256]{1,0:T(2,128)S(1)} fusion(bf16[2,256,256]{2,1,0:T(8,128)(2,1)} %param.11), kind=kLoop, calls=%fused_computation.45 | loop fusion | flops 392704 | bytes 264192 | tf_op jit(solution)/shard_map/reduce_sum | solution.py:23
  1.2 1.1 %fusion.35 = bf16[2,256,256]{2,1,0:T(8,128)(2,1)S(1)} fusion(bf16[2,256,256]{2,1,0:T(8,128)(2,1)} %param.11, f32[2,256]{1,0:T(2,128)S(1)} %add_rsqrt_fusion.6), kind=kLoop, calls=%fused_computation.46 | loop fusion | flops 393216 | bytes 526336 | tf_op jit(solution)/shard_map/convert_element_type | solution.py:119
  2.3 0.7 fusion.71
  3.0 2.4 %collective-permute-start.1 = (bf16[2,128,256]{2,1,0:T(8,128)(2,1)}, bf16[2,128,256]{2,1,0:T(8,128)(2,1)}, u32[]{:S(2)}, u32[]{:S(2)}) collective-permute-start(bf16[2,128,256]{2,1,0:T(8,128)(2,1)} %get-tuple-element.50), channel_id=1, source_target_pairs={{8,0},{16,8},{24,16},{0,24},{9,1},{17,9},{25,17},{1,25},{10,2},{18... | collective-permute-start | bytes 393224 | tf_op jit(solution)/shard_map/ppermute | solution.py:17
  5.4 1.4 %fusion.40 = f32[2,256,768]{2,1,0:T(8,128)S(1)} fusion(bf16[2,256,256]{2,1,0:T(8,128)(2,1)S(1)} %fusion.35, bf16[256,768]{1,0:T(8,128)(2,1)} %param.14), kind=kOutput, calls=%fused_computation.76 | convolution fusion | flops 201326592 | bytes 2228224 | tf_op jit(solution)/shard_map/dot_general | solution.py:120
  6.9 0.7 slice.108
  7.6 1.1 %slice_multiply_fusion.2 = (f32[2,256,256]{2,1,0:T(8,128)}, f32[2,256,256]{2,1,0:T(8,128)}) fusion(f32[2,256,768]{2,1,0:T(8,128)S(1)} %fusion.40), kind=kLoop, calls=%fused_computation.69 | loop fusion | flops 262144 | bytes 2097152 | tf_op jit(solution)/shard_map/mul | solution.py:29
  8.8 0.5 reshape.240
  9.3 0.1 slice_compare_fusion
  9.4 0.8 eq.47
  10.2 0.8 eq.49
  11.1 0.1 dynamic_slice.11
  11.1 1.2 %copy.104 = f32[2,256,256]{1,2,0:T(8,128)S(1)} copy(f32[2,256,256]{2,1,0:T(8,128)} %get-tuple-element.29) | data formatting | bytes 1048576 | tf_op jit(solution)/shard_map/mul | solution.py:29
  12.5 0.2 copy.105
  12.7 1.2 %copy.99 = f32[2,256,256]{1,2,0:T(8,128)S(1)} copy(f32[2,256,256]{2,1,0:T(8,128)} %get-tuple-element.40) | data formatting | bytes 1048576 | tf_op jit(solution)/shard_map/mul | solution.py:29
  14.1 0.8 mul.177
  14.9 1.3 %copy.100 = f32[2,256,256]{2,1,0:T(8,128)S(1)} copy(f32[2,256,256]{1,2,0:T(8,128)} %bitcast.87) | data formatting | bytes 1048576 | tf_op jit(solution)/shard_map/mul | solution.py:30
  16.2 0.9 multiply_convert_fusion.2
  17.1 1.8 %copy.101 = bf16[2,256,256]{1,2,0:T(8,128)(2,1)} copy(bf16[2,256,256]{2,1,0:T(8,128)(2,1)} %get-tuple-element.28) | data formatting | bytes 524288 | tf_op jit(solution)/shard_map/convert_element_type | solution.py:124
  18.9 0.1 fusion.54
  19.0 1.8 %and_or_fusion = pred[256,512]{1,0:T(8,128)(4,1)} fusion(pred[256,512]{1,0:T(8,128)(4,1)} %eq.47, pred[256,512]{1,0:T(8,128)(4,1)} %eq.49, s32[512]{0:T(512)S(1)} %fusion.54, s32[256]{0:T(256)S(1)} %dynamic_slice.11), kind=kLoop, calls=%fused_computation.66 | loop fusion | flops 393216 | bytes 396288 | tf_op jit(solution)/shard_map/while/body/eval_jaxpr/or | solution.py:43
  20.8 0.7 broadcast_multiply_fusion.1
  21.5 1.3 %fusion.73 = (bf16[2,256,512]{2,1,0:T(8,128)(2,1)S(1)}, f32[2,256,512]{2,1,0:T(8,128)S(1)}) fusion(bf16[256,768]{1,0:T(8,128)(2,1)S(1)} %copy-done.2, bf16[2,128,256]{2,1,0:T(8,128)(2,1)} %collective-permute-done.1, bf16[2,128,256]{2,1,0:T(8,128)(2,1)} %collective-permute-done), kind=kOutput, calls=%fused_computation.116 | convolution fusion | flops 135004160 | bytes 2097152 | tf_op jit(solution)/shard_map/dot_general | solution.py:129
  22.9 0.2 copy.98
  23.1 0.2 copy.102
  23.5 0.2 copy.103
  23.7 0.1 multiply_convert_fusion.3
  23.8 0.5 copy-done.4
  24.3 0.2 copy.106
  24.5 0.1 copy-done.8
  24.7 5.2 %fusion.74 = (f32[2,8,256]{2,1,0:T(8,128)S(1)}, f32[2,8,256,512]{3,2,1,0:T(8,128)}) fusion(f32[8]{0:T(128)S(1)} %broadcast_multiply_fusion.1, pred[256,512]{1,0:T(8,128)(4,1)S(1)} %copy-done.11, bf16[2,256,8,32]{1,3,2,0:T(8,128)(2,1)S(1)} %bitcast.95, bf16[2,512,8,32]{1,3,2,0:T(8,128)(2,1)S(1)} %bitcast.92), kind=kOutput, calls=%fused_computation.117 | convolution fusion | flops 142606848 | bytes 9322528 | tf_op jit(solution)/shard_map/while/body/eval_jaxpr/sub | solution.py:48
  29.9 4.9 %fusion.20 = bf16[2,8,32,256]{3,2,1,0:T(8,128)(2,1)S(1)} fusion(bf16[2,512,8,32]{1,3,2,0:T(8,128)(2,1)S(1)} %bitcast.91, f32[2,8,256,512]{3,2,1,0:T(8,128)} %get-tuple-element.56, f32[2,8,256]{2,1,0:T(8,128)S(1)} %get-tuple-element.55), kind=kOutput, calls=%fused_computation.30 | convolution fusion | flops 138543104 | bytes 9191424 | tf_op jit(solution)/shard_map/while/body/eval_jaxpr/mhqk,mkhd->mqhd/dot_general | solution.py:50
  34.8 0.3 fusion.18
  35.1 0.7 copy.108
  35.8 5.8 %all-to-all-start = ((bf16[2,8,32,256]{3,2,0,1:T(8,128)(2,1)}), bf16[2,8,32,256]{3,2,0,1:T(8,128)(2,1)S(1)}, u32[]{:S(2)}, u32[]{:S(2)}) async-start(bf16[2,8,32,256]{3,2,0,1:T(8,128)(2,1)} %copy.108), calls=%async_computation | async-start | bytes 524288 | tf_op jit(solution)/shard_map/all_to_all | solution.py:167
  41.6 9.7 %all-to-all-done = bf16[2,8,32,256]{3,2,0,1:T(8,128)(2,1)S(1)} async-done(((bf16[2,8,32,256]{3,2,0,1:T(8,128)(2,1)}), bf16[2,8,32,256]{3,2,0,1:T(8,128)(2,1)S(1)}, u32[]{:S(2)}, u32[]{:S(2)}) %all-to-all-start) | async-done | bytes 262176 | tf_op jit(solution)/shard_map/all_to_all | solution.py:167
  51.3 0.2 multiply_reduce_fusion.2
  51.5 0.1 fusion.37
  51.7 0.4 fusion.38
  52.1 0.1 slice_multiply_fusion.1
  52.2 0.8 slice.107
  53.0 1.8 %mul.196 = f32[16,32,8,32]{3,2,1,0:T(8,128)} reshape(f32[16,32,256]{2,1,0:T(8,128)S(1)} %get-tuple-element.25) | data formatting | bytes 1048576 | tf_op jit(solution)/shard_map/mul | solution.py:29
  54.8 2.2 %reduce_sum.99 = f32[16,32,8]{2,1,0:T(8,128)S(1)} reduce(f32[16,32,8,32]{3,2,1,0:T(8,128)} %mul.196, f32[]{:T(128)} %constant.23.clone.1), dimensions={3}, to_apply=%region_7.8 | reduce | flops 126976 | bytes 540676 | tf_op jit(solution)/shard_map/reduce_sum | solution.py:29
  57.1 2.0 %mul.197 = f32[16,32,8,32]{3,2,1,0:T(8,128)} broadcast(f32[16,32,8]{2,1,0:T(8,128)S(1)} %add_rsqrt_fusion.1), dimensions={0,1,2} | broadcast | bytes 540672 | tf_op jit(solution)/shard_map/mul | solution.py:30
  59.0 2.1 %mul.198 = f32[16,32,256]{2,1,0:T(8,128)S(1)} reshape(f32[16,32,8,32]{3,2,1,0:T(8,128)} %mul.197) | data formatting | bytes 1048576 | tf_op jit(solution)/shard_map/mul | solution.py:30
  61.2 1.8 %mul.201 = f32[16,32,8,32]{3,2,1,0:T(8,128)} reshape(f32[16,32,256]{2,1,0:T(8,128)S(1)} %get-tuple-element.26) | data formatting | bytes 1048576 | tf_op jit(solution)/shard_map/mul | solution.py:29
  63.0 2.2 %reduce_sum.100 = f32[16,32,8]{2,1,0:T(8,128)S(1)} reduce(f32[16,32,8,32]{3,2,1,0:T(8,128)} %mul.201, f32[]{:T(128)} %constant.23.clone.1), dimensions={3}, to_apply=%region_8.9 | reduce | flops 126976 | bytes 540676 | tf_op jit(solution)/shard_map/reduce_sum | solution.py:29
  65.3 2.0 %mul.202 = f32[16,32,8,32]{3,2,1,0:T(8,128)} broadcast(f32[16,32,8]{2,1,0:T(8,128)S(1)} %add_rsqrt_fusion), dimensions={0,1,2} | broadcast | bytes 540672 | tf_op jit(solution)/shard_map/mul | solution.py:30
  67.2 2.1 %mul.203 = f32[16,32,256]{2,1,0:T(8,128)S(1)} reshape(f32[16,32,8,32]{3,2,1,0:T(8,128)} %mul.202) | data formatting | bytes 1048576 | tf_op jit(solution)/shard_map/mul | solution.py:30
  69.4 0.9 multiply_convert_fusion.1
  70.3 1.7 %reshape.246 = bf16[16,32,8,32]{3,2,1,0:T(8,128)(2,1)S(1)} reshape(bf16[16,32,256]{2,1,0:T(8,128)(2,1)} %get-tuple-element.24) | data formatting | bytes 524288 | tf_op jit(solution)/shard_map/reshape | solution.py:70
  72.0 2.4 %reshape.245 = bf16[16,32,8,32]{3,2,1,0:T(8,128)(2,1)} reshape(bf16[16,32,256]{2,1,0:T(8,128)(2,1)} %get-tuple-element.23) | data formatting | bytes 524288 | tf_op jit(solution)/shard_map/reshape | solution.py:65
  74.4 0.4 reshape.244
  74.9 4.5 %fusion.75 = (f32[32,8,16]{2,1,0:T(8,128)S(1)}, f32[32,8,16,16]{2,3,1,0:T(8,128)}) fusion(f32[8]{0:T(128)S(1)} %broadcast_multiply_fusion, bf16[16,32,8,32]{3,2,1,0:T(8,128)(2,1)S(1)} %reshape.246, bf16[16,32,8,32]{3,2,1,0:T(8,128)(2,1)} %reshape.245), kind=kOutput, calls=%fused_computation.118 | convolution fusion | flops 4390927 | bytes 802848 | tf_op jit(solution)/shard_map/sub | solution.py:77
  79.3 2.5 %fusion.16 = bf16[16,32,8,32]{3,0,2,1:T(8,128)(2,1)S(1)} fusion(f32[32,8,16,16]{2,3,1,0:T(8,128)} %get-tuple-element.58, bf16[16,32,8,32]{3,2,1,0:T(8,128)(2,1)S(1)} %reshape.244, f32[32,8,16]{2,1,0:T(8,128)S(1)} %get-tuple-element.57), kind=kOutput, calls=%fused_computation.24 | convolution fusion | flops 4456448 | bytes 802816 | tf_op jit(solution)/shard_map/phmn,nphd->mphd/dot_general | solution.py:79
  81.8 0.3 copy.115
  82.1 0.7 convert_element_type.136
  82.9 0.2 fusion.21
  83.1 12.5 %all_to_all.8 = bf16[16,1,32,256]{3,2,1,0:T(8,128)(2,1)S(1)} all-to-all(bf16[16,1,32,256]{3,2,1,0:T(8,128)(2,1)S(1)} %fusion.21), channel_id=1, replica_groups=mesh['sector'=4,'member'=8] {'member'}, dimensions={0} | all-to-all | bytes 524288 | tf_op jit(solution)/shard_map/all_to_all | solution.py:173
  95.7 0.1 multiply_reduce_fusion.1
  95.9 0.1 rsqrt.79
  96.0 0.1 fusion.36
  96.1 1.0 fusion.17
  97.1 0.8 add_convert_fusion
  (58 shorter events, 0.9 us)
Async XLA Ops:
  0.0 96.1 %copy-start = (bf16[1024,256]{1,0:T(8,128)(2,1)S(1)}, bf16[1024,256]{1,0:T(8,128)(2,1)}, u32[]{:S(2)}) copy-start(bf16[1024,256]{1,0:T(8,128)(2,1)} %param.21) | copy-start | bytes 1572868
  3.0 18.5 %collective-permute-start.1 = (bf16[2,128,256]{2,1,0:T(8,128)(2,1)}, bf16[2,128,256]{2,1,0:T(8,128)(2,1)}, u32[]{:S(2)}, u32[]{:S(2)}) collective-permute-start(bf16[2,128,256]{2,1,0:T(8,128)(2,1)} %get-tuple-element.50), channel_id=1, source_target_pairs={{8,0},{16,8},{24,16},{0,24},{9,1},{17,9},{25,17},{1,25},{10,2},{18... | collective-permute-start | bytes 393224 | tf_op jit(solution)/shard_map/ppermute | solution.py:17
  5.4 16.1 %collective-permute-start = (bf16[2,128,256]{2,1,0:T(8,128)(2,1)}, bf16[2,128,256]{2,1,0:T(8,128)(2,1)}, u32[]{:S(2)}, u32[]{:S(2)}) collective-permute-start(bf16[2,128,256]{2,1,0:T(8,128)(2,1)} %get-tuple-element.49), channel_id=1, source_target_pairs={{0,8},{8,16},{16,24},{24,0},{1,9},{9,17},{17,25},{25,1},{2,10},{10... | collective-permute-start | bytes 393224 | tf_op jit(solution)/shard_map/ppermute | solution.py:16
  5.4 3.2 %copy-start.7 = (s32[256,256]{1,0:T(8,128)S(1)}, s32[256,256]{1,0:T(8,128)}, u32[]{:S(2)}) copy-start(s32[256,256]{1,0:T(8,128)} %param.12) | copy-start | bytes 786436
  8.7 2.4 %copy-start.12 = (s32[1024]{0:T(1024)S(1)}, s32[1024]{0:T(1024)}, u32[]{:S(2)}) copy-start(s32[1024]{0:T(1024)} %param.13) | copy-start | bytes 12292
  14.9 6.6 %copy-start.2 = (bf16[256,768]{1,0:T(8,128)(2,1)S(1)}, bf16[256,768]{1,0:T(8,128)(2,1)}, u32[]{:S(2)}) copy-start(bf16[256,768]{1,0:T(8,128)(2,1)} %param.14) | copy-start | bytes 1179652
  17.1 5.7 %copy-start.5 = (bf16[2,256,256]{2,1,0:T(8,128)(2,1)S(1)}, bf16[2,256,256]{2,1,0:T(8,128)(2,1)}, u32[]{:S(2)}) copy-start(bf16[2,256,256]{2,1,0:T(8,128)(2,1)} %slice.108) | copy-start | bytes 786436
  23.3 1.0 copy-start.4
  23.7 1.0 copy-start.8
  23.7 1.0 %copy-start.11 = (pred[256,512]{1,0:T(8,128)(4,1)S(1)}, pred[256,512]{1,0:T(8,128)(4,1)}, u32[]{:S(2)}) copy-start(pred[256,512]{1,0:T(8,128)(4,1)} %and_or_fusion) | copy-start | bytes 393220
  29.9 4.9 %copy-start.1 = (bf16[2,256,256]{2,1,0:T(8,128)(2,1)S(1)}, bf16[2,256,256]{2,1,0:T(8,128)(2,1)}, u32[]{:S(2)}) copy-start(bf16[2,256,256]{2,1,0:T(8,128)(2,1)} %param.11) | copy-start | bytes 786436
  29.9 4.9 %copy-start.9 = (bf16[256,256]{1,0:T(8,128)(2,1)S(1)}, bf16[256,256]{1,0:T(8,128)(2,1)}, u32[]{:S(2)}) copy-start(bf16[256,256]{1,0:T(8,128)(2,1)} %param.15) | copy-start | bytes 393220
  29.9 11.7 %copy-start.14 = (f32[8]{0:T(128)S(1)}, f32[8]{0:T(128)}, u32[]{:S(2)}) copy-start(f32[8]{0:T(128)} %param.19) | copy-start | bytes 100
  34.7 16.9 %copy-start.6 = (bf16[256,768]{1,0:T(8,128)(2,1)S(1)}, bf16[256,768]{1,0:T(8,128)(2,1)}, u32[]{:S(2)}) copy-start(bf16[256,768]{1,0:T(8,128)(2,1)} %param.17) | copy-start | bytes 1179652
  35.8 15.6 %all-to-all-start = ((bf16[2,8,32,256]{3,2,0,1:T(8,128)(2,1)}), bf16[2,8,32,256]{3,2,0,1:T(8,128)(2,1)S(1)}, u32[]{:S(2)}, u32[]{:S(2)}) async-start(bf16[2,8,32,256]{3,2,0,1:T(8,128)(2,1)} %copy.108), calls=%async_computation | async-start | bytes 524288 | tf_op jit(solution)/shard_map/all_to_all | solution.py:167
  70.3 4.2 %copy-start.3 = (bf16[16,32,256]{2,1,0:T(8,128)(2,1)S(1)}, bf16[16,32,256]{2,1,0:T(8,128)(2,1)}, u32[]{:S(2)}) copy-start(bf16[16,32,256]{2,1,0:T(8,128)(2,1)} %slice.107) | copy-start | bytes 786436
  81.8 1.1 %copy-start.10 = (bf16[256,256]{1,0:T(8,128)(2,1)S(1)}, bf16[256,256]{1,0:T(8,128)(2,1)}, u32[]{:S(2)}) copy-start(bf16[256,256]{1,0:T(8,128)(2,1)} %param.18) | copy-start | bytes 393220
  82.9 13.3 %copy-start.13 = (bf16[256,1024]{1,0:T(8,128)(2,1)S(1)}, bf16[256,1024]{1,0:T(8,128)(2,1)}, u32[]{:S(2)}) copy-start(bf16[256,1024]{1,0:T(8,128)(2,1)} %param.20) | copy-start | bytes 1572868
where the time goes:
time: 98.6 us; the launch traced here: 97.9 us
  local copies, waits for them, and re-layouts  31 us (31%)
  matrix products  21.5 us (22%)
  other arithmetic  14.4 us (15%)
  blocking collectives  12.5 us (13%)
  waiting for transfers between devices  9.75 us (10%)
  starting transfers between devices  8.24 us (8%)
    all_to_all x1, blocking collectives, on_device(): lax.all_to_all(gathered, 'member', split_axis=0, concat_axis=1, tiled=True)  12.5 us
    mul x10, local copies, waits for them, and re-layouts, head_norm(): return (shaped * lax.rsqrt(squares + 0.1)).reshape(values.shape)  10.8 us
    all_to_all x1, waiting for transfers between devices, on_device(): lax.all_to_all(regrouped, 'member', split_axis=1, concat_axis=0, tiled=True)  9.74 us
    mul x5, local copies, waits for them, and re-layouts, head_norm(): squares = jnp.mean(shaped * shaped, axis=-1, keepdims=True)  6.33 us
    all_to_all x1, starting transfers between devices, on_device(): lax.all_to_all(regrouped, 'member', split_axis=1, concat_axis=0, tiled=True)  5.81 us
    sub x1, matrix products, attend_window(): exponent = jnp.exp(scores - row_max)  5.17 us
    dot_general x1, matrix products, attend_window(): jnp.einsum('mhqk,mkhd->mqhd', weights, values, preferred_element_type=jnp...  4.87 us
    reduce_sum x5, other arithmetic, head_norm(): squares = jnp.mean(shaped * shaped, axis=-1, keepdims=True)  4.62 us
  transfers between devices with their start and end apart: 3, of which 1 were waited for; matrix products, arithmetic and copies ran while one was open for 16% of the time, Pallas kernels for 0%

commit v1 on v0

v1 whole, which is shorter than its diff:
```python
import functools
import math

import jax
import jax.numpy as jnp
from jax import lax
from jax.experimental import pallas as pl
from jax.experimental.pallas import tpu as pltpu
from jax.sharding import PartitionSpec as P

F32 = jnp.float32
BF16 = jnp.bfloat16
LANES = 128
SUB = 8
LOG2E = math.log2(math.e)
OUTSIDE = -1e30


def dot(a, b):
    return lax.dot_general(a, b, (((1,), (0,)), ((), ())), preferred_element_type=F32)


def dot_lhs_t(a, b):
    return lax.dot_general(a, b, (((0,), (0,)), ((), ())), preferred_element_type=F32)


def dot_rhs_t(a, b):
    return lax.dot_general(a, b, (((1,), (1,)), ((), ())), preferred_element_type=F32)


def rms_rows(values):
    squares = jnp.mean(values * values, axis=-1, keepdims=True)
    return (values * lax.rsqrt(squares + 1e-06)).astype(BF16)


def head_norm_lanes(values, width):
    features = values.shape[-1]
    row = lax.broadcasted_iota(jnp.int32, (features, features), 0) // width
    col = lax.broadcasted_iota(jnp.int32, (features, features), 1) // width
    block = jnp.where(row == col, 1.0, 0.0).astype(BF16)
    squares = values * values
    high = squares.astype(BF16)
    low = (squares - high.astype(F32)).astype(BF16)
    means = (dot(high, block) + dot(low, block)) * (1.0 / width)
    return (values * lax.rsqrt(means + 0.1)).astype(BF16)


def head_norm_rows(values, width):
    features, count = values.shape
    shaped = values.reshape(features // width, width, count)
    means = jnp.mean(shaped * shaped, axis=1, keepdims=True)
    return (shaped * lax.rsqrt(means + 0.1)).reshape(features, count).astype(BF16)


def attend_rows(query_t, keys, value_t, bias, scales, width):
    features, count = query_t.shape
    span = keys.shape[0]
    per_tile = LANES // width
    ones = jnp.ones((16, span), BF16)
    mixed = []
    for first in range(0, features // width, 2):
        tile = first // per_tile
        tile_keys = keys[:, tile * LANES : (tile + 1) * LANES]
        padded = []
        for head in (first, first + 1):
            above = (head % per_tile) * width
            parts = []
            if above:
                parts.append(jnp.zeros((above, count), BF16))
            parts.append(query_t[head * width : (head + 1) * width])
            if LANES - above - width:
                parts.append(jnp.zeros((LANES - above - width, count), BF16))
            padded.append(jnp.concatenate(parts, axis=0))
        scores = dot(tile_keys, jnp.concatenate(padded, axis=1))
        powers = []
        for i in range(2):
            mine = scores[:, i * count : (i + 1) * count] + bias
            top = jnp.max(mine, axis=0, keepdims=True)
            powers.append(jnp.exp2((mine - top) * scales[first + i]).astype(BF16))
        left = jnp.concatenate([value_t[first * width : (first + 2) * width], ones], axis=0)
        both = dot(left, jnp.concatenate(powers, axis=1))
        for i in range(2):
            columns = slice(i * count, (i + 1) * count)
            total = both[2 * width : 2 * width + 1, columns]
            mixed.append(both[i * width : (i + 1) * width, columns] * (1.0 / total))
    return jnp.concatenate(mixed, axis=0)


def project_kernel(
    width, radius, state_ref, mask_ref, window_ref, weight_ref, key_ref, query_ref, value_ref, bias_ref
):
    members, tokens, features = state_ref.shape
    rows = members * tokens
    normed = rms_rows(state_ref[...].reshape(rows, features).astype(F32))
    key_ref[...] = head_norm_lanes(
        dot(normed, weight_ref[:, features : 2 * features]), width
    ).reshape(members, tokens, features)
    query_w = weight_ref[:, :features].T
    value_w = weight_ref[:, 2 * features :].T
    query_t = head_norm_rows(dot_rhs_t(query_w, normed), width)
    value_t = dot_rhs_t(value_w, normed).astype(BF16)
    for m in range(members):
        query_ref[m] = query_t[:, m * tokens : (m + 1) * tokens]
        value_ref[m] = value_t[:, m * tokens : (m + 1) * tokens]

    tiles = window_ref.shape[0]
    span = LANES + 2 * radius
    base = lax.axis_index("sector") * (tokens // LANES)
    for block in range(tokens // LANES):
        table = mask_ref[block * LANES : (block + 1) * LANES, :] + 1
        table = jnp.concatenate([table, jnp.zeros((LANES, span - 2 * radius), jnp.int32)], axis=1)
        banded = pltpu.roll(table, 0, 1, stride=1, stride_axis=0)
        own = jnp.broadcast_to(window_ref[pl.ds(base + block, 1), :], (LANES, LANES)).T
        for part in range(span // LANES):
            index = lax.rem(base + (tiles + block + part - radius // LANES), tiles)
            theirs = window_ref[pl.ds(index, 1), :]
            piece = banded[:, part * LANES : (part + 1) * LANES]
            allowed = (piece == 2) | ((piece == 1) & (own == theirs))
            bias = jnp.where(allowed, 0.0, OUTSIDE)
            bias_ref[block, part * LANES : (part + 1) * LANES, :] = bias.T


def window_kernel(
    width,
    share,
    state_ref,
    before_ref,
    after_ref,
    weight_ref,
    out_weight_ref,
    heat_ref,
    key_ref,
    query_ref,
    value_ref,
    bias_ref,
    parcel_ref,
):
    members, tokens, features = state_ref.shape
    radius = before_ref.shape[1]
    blocks = tokens // LANES
    span = bias_ref.shape[1]
    heads = features // width
    scales = [heat_ref[h] * (LOG2E / math.sqrt(width)) for h in range(heads)]
    edges = jnp.concatenate(
        [r[m] for m in range(members) for r in (before_ref, after_ref)], axis=0
    )
    normed = rms_rows(edges.astype(F32))
    edge_key = head_norm_lanes(dot(normed, weight_ref[:, features : 2 * features]), width)
    edge_value = dot_rhs_t(weight_ref[:, 2 * features :].T, normed).astype(BF16)
    results = []
    for m in range(members):
        at = 2 * m * radius
        keys = jnp.concatenate(
            [edge_key[at : at + radius], key_ref[m], edge_key[at + radius : at + 2 * radius]], axis=0
        )
        value_t = jnp.concatenate(
            [
                edge_value[:, at : at + radius],
                value_ref[m],
                edge_value[:, at + radius : at + 2 * radius],
            ],
            axis=1,
        )
        mixed = []
        for block in range(blocks):
            low = block * LANES
            mixed.append(
                attend_rows(
                    query_ref[m, :, low : low + LANES],
                    keys[low : low + span],
                    value_t[:, low : low + span],
                    bias_ref[block],
                    scales,
                    width,
                )
            )
        mixed = jnp.concatenate(mixed, axis=1).T.astype(BF16)
        results.append(state_ref[m].astype(F32) + dot(mixed, out_weight_ref[...]))
    parts = [r.reshape(tokens // SUB, 1, SUB, features) for r in results]
    packed = jnp.concatenate(parts, axis=1).reshape(members * tokens, features)
    parcel_ref[...] = packed.astype(BF16).reshape(parcel_ref.shape)


def member_kernel(
    width, parcel_ref, weight_ref, out_weight_ref, heat_ref, up_ref, down_ref, result_ref
):
    sources, groups, rows, features = parcel_ref.shape
    held = rows // SUB
    size = sources * rows
    heads = features // width
    scales = [heat_ref[h] * (LOG2E / math.sqrt(width)) for h in range(heads)]
    state = jnp.concatenate(
        [parcel_ref[:, g].reshape(size, features) for g in range(groups)], axis=0
    ).astype(F32)
    normed = rms_rows(state)
    keys = head_norm_lanes(dot(normed, weight_ref[:, features : 2 * features]), width)
    query_t = head_norm_rows(dot_rhs_t(weight_ref[:, :features].T, normed), width)
    value_t = dot_rhs_t(weight_ref[:, 2 * features :].T, normed).astype(BF16)
    key_patch = lax.rem(lax.broadcasted_iota(jnp.int32, (size, LANES), 0), SUB)
    query_patch = lax.rem(lax.broadcasted_iota(jnp.int32, (size, LANES), 1), SUB)
    bias = jnp.where(key_patch == query_patch, 0.0, OUTSIDE)
    mixed = []
    for g in range(groups):
        span = slice(g * size, (g + 1) * size)
        for low in range(g * size, (g + 1) * size, LANES):
            mixed.append(
                attend_rows(
                    query_t[:, low : low + LANES], keys[span], value_t[:, span], bias, scales, width
                )
            )
    mixed = jnp.concatenate(mixed, axis=1).T.astype(BF16)
    state = (state + dot(mixed, out_weight_ref[...])).astype(BF16).astype(F32)
    hidden = jax.nn.gelu(dot(rms_rows(state), up_ref[...])).astype(BF16)
    state = state + dot(hidden, down_ref[...])
    state = state.reshape(groups, sources, held, SUB, features)
    pieces = [
        state[g, s, m] for s in range(sources) for m in range(held) for g in range(groups)
    ]
    state = jnp.concatenate(pieces, axis=0).astype(BF16)
    result_ref[...] = state.reshape(result_ref.shape)


VMEM = pl.BlockSpec(memory_space=pltpu.VMEM)
SMEM = pl.BlockSpec(memory_space=pltpu.SMEM)


def on_device(
    state,
    window_mask,
    window_index,
    w_space_qkv,
    w_space_out,
    temp_space,
    w_ens_qkv,
    w_ens_out,
    temp_ens,
    w_in,
    w_out,
):
    members, tokens, features = state.shape
    width = features // temp_space.shape[0]
    radius = window_mask.shape[1] // 2
    sectors = lax.axis_size("sector")
    ring = [(i, (i + 1) % sectors) for i in range(sectors)]
    back = [(j, i) for i, j in ring]
    before = lax.ppermute(state[:, tokens - radius :], "sector", ring)
    after = lax.ppermute(state[:, :radius], "sector", back)
    blocks = tokens // LANES
    span = LANES + 2 * radius
    key, query, value, bias = pl.pallas_call(
        functools.partial(project_kernel, width, radius),
        out_shape=(
            jax.ShapeDtypeStruct((members, tokens, features), BF16),
            jax.ShapeDtypeStruct((members, features, tokens), BF16),
            jax.ShapeDtypeStruct((members, features, tokens), BF16),
            jax.ShapeDtypeStruct((blocks, span, LANES), F32),
        ),
        in_specs=[VMEM] * 4,
        out_specs=(VMEM,) * 4,
        name="project",
        cost_estimate=pl.CostEstimate(flops=10**9, transcendentals=0, bytes_accessed=10**6),
    )(state, window_mask, window_index.reshape(-1, LANES), w_space_qkv)

    group_size = lax.axis_size("member")
    share = tokens // group_size
    groups = share // SUB
    parcel = pl.pallas_call(
        functools.partial(window_kernel, width, share),
        out_shape=jax.ShapeDtypeStruct((group_size, groups, members * SUB, features), BF16),
        in_specs=[VMEM] * 5 + [SMEM] + [VMEM] * 4,
        out_specs=VMEM,
        name="window",
        cost_estimate=pl.CostEstimate(flops=10**9, transcendentals=0, bytes_accessed=10**6),
    )(state, before, after, w_space_qkv, w_space_out, temp_space, key, query, value, bias)
    parcel = lax.all_to_all(parcel, "member", split_axis=0, concat_axis=0, tiled=True)
    result = pl.pallas_call(
        functools.partial(member_kernel, width),
        out_shape=jax.ShapeDtypeStruct((group_size, members, share, features), BF16),
        in_specs=[VMEM] * 3 + [SMEM] + [VMEM] * 2,
        out_specs=VMEM,
        name="member",
        cost_estimate=pl.CostEstimate(flops=10**9, transcendentals=0, bytes_accessed=10**6),
    )(parcel, w_ens_qkv, w_ens_out, temp_ens, w_in, w_out)
    result = lax.all_to_all(result, "member", split_axis=0, concat_axis=0, tiled=True)
    return jnp.swapaxes(result, 0, 1).reshape(members, tokens, features)


def solution(mesh):
    return jax.shard_map(
        on_device,
        mesh=mesh,
        in_specs=(
            P("member", "sector", None),
            P("sector", None),
            P(),
            P(),
            P(),
            P(),
            P(),
            P(),
            P(),
            P(),
            P(),
        ),
        out_specs=P("member", "sector", None),
        check_vma=False,
    )
```

time: 98.6 us -> 52.1 us (0.53)
  local copies, waits for them, and re-layouts: 31 us -> 2.35 us
  matrix products: 21.5 us -> 0 us
  Pallas kernels: 0 us -> 18.2 us
  other arithmetic: 14.4 us -> 0 us
  blocking collectives: 12.5 us -> 26.4 us
  waiting for transfers between devices: 9.75 us -> 2.18 us
  starting transfers between devices: 8.24 us -> 2.49 us
    pallas_call x0 -> x3, Pallas kernels: none -> 18.2 us  [the longest x1 8.31 us: on_device(): pl.pallas_call(functools.partial(window_kernel, width, share), out_shape=...]
    mul x15 -> x0, local copies, waits for them, and re-layouts: 17.1 us -> none  [the longest x10 10.8 us: head_norm(): return (shaped * lax.rsqrt(squares + 0.1)).reshape(values.shape)]
    all_to_all x1 -> x2, blocking collectives: 12.5 us -> 26.4 us  [the longest x1 14.4 us: on_device(): lax.all_to_all(parcel, 'member', split_axis=0, concat_axis=0, tiled=True)]
    dot_general x8 -> x0, matrix products: 11.8 us -> none  [the longest x1 4.87 us: attend_window(): jnp.einsum('mhqk,mkhd->mqhd', weights, values, preferred_element_type=jnp...]
    all_to_all x1 -> x0, waiting for transfers between devices: 9.74 us -> none  [on_device(): lax.all_to_all(regrouped, 'member', split_axis=1, concat_axis=0, tiled=True)]
    sub x2 -> x0, matrix products: 9.63 us -> none  [the longest x1 5.17 us: attend_window(): exponent = jnp.exp(scores - row_max)]
    reduce_sum x8 -> x0, other arithmetic: 6.06 us -> none  [the longest x5 4.62 us: head_norm(): squares = jnp.mean(shaped * shaped, axis=-1, keepdims=True)]
    reshape x5 -> x0, local copies, waits for them, and re-layouts: 5.81 us -> none  [the longest x1 2.45 us: member_attention_step(): head_norm(projected[..., :features], total_heads).astype(jnp.bfloat16)]
  transfers between devices with their start and end apart: 3 -> 2, of which waited for: 1 -> 2; matrix products, arithmetic and copies ran while one was open for 16% -> 0% of each run, Pallas kernels for 0% -> 5%
where the time goes in v1:
time: 52.1 us; the launch traced here: 51.6 us
  blocking collectives  26.4 us (51%)
  Pallas kernels  18.2 us (35%)
  starting transfers between devices  2.49 us (5%)
  local copies, waits for them, and re-layouts  2.35 us (5%)
  waiting for transfers between devices  2.18 us (4%)
    all_to_all x1, blocking collectives, on_device(): lax.all_to_all(parcel, 'member', split_axis=0, concat_axis=0, tiled=True)  14.4 us
    all_to_all x1, blocking collectives, on_device(): lax.all_to_all(result, 'member', split_axis=0, concat_axis=0, tiled=True)  12 us
    pallas_call x1, Pallas kernels, on_device(): pl.pallas_call(functools.partial(window_kernel, width, share), out_shape=...  8.31 us
    pallas_call x1, Pallas kernels, on_device(): pl.pallas_call(functools.partial(member_kernel, width), out_shape=jax.Sha...  7.19 us
    pallas_call x1, Pallas kernels, on_device(): pl.pallas_call(functools.partial(project_kernel, width, radius), out_shap...  2.73 us
    ppermute x1, starting transfers between devices, on_device(): after = lax.ppermute(state[:, :radius], 'sector', back)  2.49 us
    ppermute x1, waiting for transfers between devices, on_device(): after = lax.ppermute(state[:, :radius], 'sector', back)  1.1 us
    ppermute x1, waiting for transfers between devices, on_device(): before = lax.ppermute(state[:, tokens - radius:], 'sector', ring)  1.07 us
  transfers between devices with their start and end apart: 2, of which 2 were waited for; matrix products, arithmetic and copies ran while one was open for 0% of the time, Pallas kernels for 5%

profile of v1, /device:TPU:0, one launch (start us, length us, event | category | flops | bytes accessed | tf_op | source)
XLA Modules:
  0.0 51.6 jit_solution(16638866186798809374)
XLA Ops:
  0.0 1.0 %fusion = (bf16[2,128,256]{2,1,0:T(8,128)(2,1)S(1)}, bf16[2,128,256]{2,1,0:T(8,128)(2,1)S(1)}) fusion(bf16[2,256,256]{2,1,0:T(8,128)(2,1)} %state_ref.3), kind=kLoop, calls=%fused_computation | loop fusion | bytes 524288 | tf_op jit(solution)/shard_map/slice | solution.py:247
  1.0 2.5 %collective-permute-start.1 = (bf16[2,128,256]{2,1,0:T(8,128)(2,1)S(1)}, bf16[2,128,256]{2,1,0:T(8,128)(2,1)S(1)}, u32[]{:S(2)}, u32[]{:S(2)}) collective-permute-start(bf16[2,128,256]{2,1,0:T(8,128)(2,1)S(1)} %get-tuple-element.13), channel_id=1, source_target_pairs={{8,0},{16,8},{24,16},{0,24},{9,1},{17,9},{25,17},{1,25},{10,2},{18... | collective-permute-start | bytes 393224 | tf_op jit(solution)/shard_map/ppermute | solution.py:247
  3.5 0.0 collective-permute-start
  3.5 2.7 %project.1 = (bf16[2,256,256]{2,1,0:T(8,128)(2,1)}, bf16[2,256,256]{2,1,0:T(8,128)(2,1)}, bf16[2,256,256]{2,1,0:T(8,128)(2,1)}, f32[2,384,128]{2,1,0:T(8,128)}) custom-call(bf16[2,256,256]{2,1,0:T(8,128)(2,1)} %state_ref.3, s32[256,256]{1,0:T(8,128)} %mask_ref.1, s32[8,128]{1,0:T(8,128)} %bitcast.4, bf16[256,768]{1,0:T(8,128)(2,1)} %weight_ref.4), custom_call_target="tpu_custom_call" | custom-call | flops 1000000000 | bytes 1000000 | tf_op jit(solution)/shard_map/project/pallas_call | solution.py:250
  6.2 1.1 %collective-permute-done.1.after_ref = bf16[2,128,256]{2,1,0:T(8,128)(2,1)S(1)} collective-permute-done((bf16[2,128,256]{2,1,0:T(8,128)(2,1)S(1)}, bf16[2,128,256]{2,1,0:T(8,128)(2,1)S(1)}, u32[]{:S(2)}, u32[]{:S(2)}) %collective-permute-start.1) | collective-permute-done | bytes 131104 | tf_op jit(solution)/shard_map/ppermute | solution.py:247
  7.3 0.0 copy-start
  7.3 1.1 %collective-permute-done.before_ref = bf16[2,128,256]{2,1,0:T(8,128)(2,1)S(1)} collective-permute-done((bf16[2,128,256]{2,1,0:T(8,128)(2,1)S(1)}, bf16[2,128,256]{2,1,0:T(8,128)(2,1)S(1)}, u32[]{:S(2)}, u32[]{:S(2)}) %collective-permute-start) | collective-permute-done | bytes 131104 | tf_op jit(solution)/shard_map/ppermute | solution.py:246
  8.4 0.0 copy-start.1
  8.4 0.0 copy-done
  8.4 0.6 %copy-done.1 = bf16[2,128,256]{2,1,0:T(8,128)(2,1)} copy-done((bf16[2,128,256]{2,1,0:T(8,128)(2,1)}, bf16[2,128,256]{2,1,0:T(8,128)(2,1)S(1)}, u32[]{:S(2)}) %copy-start.1) | copy-done | bytes 131096
  9.0 8.3 %window.1 = bf16[8,4,16,256]{3,2,1,0:T(8,128)(2,1)} custom-call(bf16[2,256,256]{2,1,0:T(8,128)(2,1)} %state_ref.3, bf16[2,128,256]{2,1,0:T(8,128)(2,1)} %copy-done.1, bf16[2,128,256]{2,1,0:T(8,128)(2,1)} %copy-done, bf16[256,768]{1,0:T(8,128)(2,1)} %weight_ref.4, bf16[256,256]{1,0:T(8,128)(2,1)} %out_weight_ref.2, f32[8]{0:T(128)} %heat_ref.2, ...), custom_call_target="tpu_custom_call" | custom-call | flops 1000000000 | bytes 1000000 | tf_op jit(solution)/shard_map/window/pallas_call | solution.py:267
  17.4 14.4 %all_to_all.10.parcel_ref = bf16[8,4,16,256]{3,2,1,0:T(8,128)(2,1)} all-to-all(bf16[8,4,16,256]{3,2,1,0:T(8,128)(2,1)} %window.1), channel_id=1, replica_groups=mesh['sector'=4,'member'=8] {'member'}, dimensions={0} | all-to-all | bytes 524288 | tf_op jit(solution)/shard_map/all_to_all | solution.py:275
  31.8 7.2 %member.1 = bf16[8,2,32,256]{3,2,1,0:T(8,128)(2,1)} custom-call(bf16[8,4,16,256]{3,2,1,0:T(8,128)(2,1)} %all_to_all.10.parcel_ref, bf16[256,768]{1,0:T(8,128)(2,1)} %weight_ref.5, bf16[256,256]{1,0:T(8,128)(2,1)} %out_weight_ref.3, f32[8]{0:T(128)} %heat_ref.3, bf16[256,1024]{1,0:T(8,128)(2,1)} %up_ref.1, bf16[1024,256]{1,0:T(8,128)(2,1)} %down_ref.1), custom_call_target="tpu_custom_call" | custom-call | flops 1000000000 | bytes 1000000 | tf_op jit(solution)/shard_map/member/pallas_call | solution.py:276
  39.0 12.0 %all_to_all.11 = bf16[8,2,32,256]{3,2,1,0:T(8,128)(2,1)S(1)} all-to-all(bf16[8,2,32,256]{3,2,1,0:T(8,128)(2,1)} %member.1), channel_id=1, replica_groups=mesh['sector'=4,'member'=8] {'member'}, dimensions={0} | all-to-all | bytes 524288 | tf_op jit(solution)/shard_map/all_to_all | solution.py:284
  50.9 0.7 %copy.12 = bf16[2,8,32,256]{3,2,1,0:T(8,128)(2,1)} copy(bf16[2,8,32,256]{3,2,0,1:T(8,128)(2,1)S(1)} %bitcast.3) | data formatting | bytes 524288 | tf_op jit(solution)/shard_map/transpose | solution.py:285
Async XLA Ops:
  1.0 6.3 %collective-permute-start.1 = (bf16[2,128,256]{2,1,0:T(8,128)(2,1)S(1)}, bf16[2,128,256]{2,1,0:T(8,128)(2,1)S(1)}, u32[]{:S(2)}, u32[]{:S(2)}) collective-permute-start(bf16[2,128,256]{2,1,0:T(8,128)(2,1)S(1)} %get-tuple-element.13), channel_id=1, source_target_pairs={{8,0},{16,8},{24,16},{0,24},{9,1},{17,9},{25,17},{1,25},{10,2},{18... | collective-permute-start | bytes 393224 | tf_op jit(solution)/shard_map/ppermute | solution.py:247
  3.5 4.9 %collective-permute-start = (bf16[2,128,256]{2,1,0:T(8,128)(2,1)S(1)}, bf16[2,128,256]{2,1,0:T(8,128)(2,1)S(1)}, u32[]{:S(2)}, u32[]{:S(2)}) collective-permute-start(bf16[2,128,256]{2,1,0:T(8,128)(2,1)S(1)} %get-tuple-element.14), channel_id=1, source_target_pairs={{0,8},{8,16},{16,24},{24,0},{1,9},{9,17},{17,25},{25,1},{2,10},{10... | collective-permute-start | bytes 393224 | tf_op jit(solution)/shard_map/ppermute | solution.py:246
  7.3 1.1 %copy-start = (bf16[2,128,256]{2,1,0:T(8,128)(2,1)}, bf16[2,128,256]{2,1,0:T(8,128)(2,1)S(1)}, u32[]{:S(2)}) copy-start(bf16[2,128,256]{2,1,0:T(8,128)(2,1)S(1)} %collective-permute-done.1.after_ref) | copy-start | bytes 393220
  8.4 0.6 %copy-start.1 = (bf16[2,128,256]{2,1,0:T(8,128)(2,1)}, bf16[2,128,256]{2,1,0:T(8,128)(2,1)S(1)}, u32[]{:S(2)}) copy-start(bf16[2,128,256]{2,1,0:T(8,128)(2,1)S(1)} %collective-permute-done.before_ref) | copy-start | bytes 393220
